TPU v7x, 128 devices: a whole 4x4x4 slice. The times are simulated.
128 devices in a mesh: lat: 16 (over z, x), lon: 4 (over y), lev: 2 (over core).
Axes of the slice: x: 4, y: 4, z: 4, core: 2. Of those that a mesh axis runs over, the one named last changes fastest.
Arguments:
- initial_heat: float32 [256, 32, 192, 128], P('lat', 'lon', 'lev'), may hold values from 0.2 to 1.8
- scaled_wind_north: float32 [256, 32, 192, 128], P('lat', 'lon', 'lev'), may hold values from -0.3 to 0.3
- scaled_wind_east: float32 [256, 32, 192, 128], P('lat', 'lon', 'lev'), may hold values from -0.3 to 0.3
- scaled_wind_vertical: float32 [256, 32, 192, 128], P('lat', 'lon', 'lev'), may hold values from -0.3 to 0.3
Outputs:
- accumulated_eastward: float32 [256, 32, 192, 128], P('lat', 'lon', 'lev')
- temperature_end: float32 [256, 32, 192, 128], P('lat', 'lon', 'lev')
All inputs are finite; a program needn't handle non-finite values.
Results may differ from a plain program's by a relative error of at most 0.00002.
Values sent between devices are 32-bit elements; how exact they have to be, the bound alone decides.
A program may use at most 448 MiB of HBM per device.

v0:
```python
import jax
import jax.numpy as jnp
from jax import lax
from jax.sharding import PartitionSpec as P

STEPS = 6


def padded(x, sides, width):
    edges = {}
    for axis, dim in sides:
        size, length = (lax.axis_size(axis), x.shape[dim])
        up = [(i, (i + 1) % size) for i in range(size - 1)]
        last = lax.slice_in_dim(x, length - width, length, axis=dim)
        leading = lax.slice_in_dim(x, 0, width, axis=dim)
        edges[dim] = (
            lax.ppermute(last, axis, up),
            lax.ppermute(leading, axis, [(b, a) for a, b in up]),
        )
    done = []
    for _, dim in sides:
        low, high = edges[dim]
        around = [(width, width) if d in done else (0, 0) for d in range(x.ndim)]
        x = jnp.concatenate([jnp.pad(low, around), x, jnp.pad(high, around)], axis=dim)
        done.append(dim)
    return x


def entering(part, axis, combine, identity):
    place = lax.axis_index(axis)
    gathered = lax.all_gather(part, axis)
    state = jnp.zeros_like(part) + jnp.asarray(identity, part.dtype)

    def one(hop, state):
        return combine(state, lax.dynamic_index_in_dim(gathered, hop, 0, False))

    return lax.fori_loop(0, place, one, state)


def strip_edges(values, dims):
    for dim in dims:
        values = lax.slice_in_dim(values, 1, values.shape[dim] - 1, axis=dim)
    return values


def neighbour(values, dim, start, dims):
    others = [other for other in dims if other != dim]
    values = strip_edges(values, others)
    return lax.slice_in_dim(values, start, start + values.shape[dim] - 2, axis=dim)


def single_update(extended_field, scaled_wind_north, scaled_wind_east, scaled_wind_vertical):
    middle = strip_edges(extended_field, (0, 1, 2))
    lower = [neighbour(extended_field, dim, 0, (0, 1, 2)) for dim in (0, 1, 2)]
    upper = [neighbour(extended_field, dim, 2, (0, 1, 2)) for dim in (0, 1, 2)]
    slopes = [above - beneath_layer for above, beneath_layer in zip(upper, lower)]
    smooth_rate = 0.05
    spread = lower[0] + upper[0] + lower[1] + upper[1] + lower[2] + upper[2] - 6.0 * middle
    return (
        middle
        - scaled_wind_north * slopes[0]
        - scaled_wind_east * slopes[1]
        - scaled_wind_vertical * slopes[2]
        + smooth_rate * spread
    )


def per_device(initial_heat, scaled_wind_north, scaled_wind_east, scaled_wind_vertical):
    for step in range(STEPS):
        extended_field = padded(initial_heat, (("lat", 0), ("lon", 1), ("lev", 2)), 1)
        initial_heat = single_update(
            extended_field, scaled_wind_north, scaled_wind_east, scaled_wind_vertical
        )
    present_layer = jnp.cumsum(initial_heat, axis=1)
    total = lax.slice_in_dim(
        present_layer, present_layer.shape[1] - 1, present_layer.shape[1], axis=1
    )

    def add_pair(earlier_total, later_total):
        return earlier_total + later_total

    beneath_layer = entering(total, "lon", add_pair, jnp.zeros_like(total))
    accumulated_eastward = (present_layer + beneath_layer) / (
        initial_heat.shape[1] * lax.axis_size("lon")
    )
    return (accumulated_eastward, initial_heat)


def solution(mesh):
    in_specs = (
        P("lat", "lon", "lev", None),
        P("lat", "lon", "lev", None),
        P("lat", "lon", "lev", None),
        P("lat", "lon", "lev", None),
    )
    out_specs = (P("lat", "lon", "lev", None), P("lat", "lon", "lev", None))
    return jax.shard_map(
        per_device, mesh=mesh, in_specs=in_specs, out_specs=out_specs, check_vma=False
    )
```

profile of v0, /device:TPU:120, one launch (start us, length us, event | category | flops | bytes accessed | tf_op | source)
XLA Modules:
  0.0 369.4 jit_solution(9412537866488740371)
XLA Ops:
  8.4 3.4 collective-permute-start.1
  17.3 4.6 %collective-permute-start = (f32[1,8,96,128]{3,2,1,0:T(8,128)S(1)}, f32[1,8,96,128]{3,2,1,0:T(8,128)S(1)}, u32[]{:S(2)}, u32[]{:S(2)}) collective-permute-start(f32[1,8,96,128]{3,2,1,0:T(8,128)S(1)} %get-tuple-element.76), channel_id=1, source_target_pairs={{8,0},{16,8},{24,16},{32,24},{40,32},{48,40},{56,48},{64,56},{72,6... | collective-permute-start | bytes 1179656 | tf_op jit(solution)/shard_map/ppermute | solution.py:18
  24.8 3.0 collective-permute-start.5
  28.6 6.5 %constant_dynamic-update-slice_fusion.1 = f32[18,8,96,128]{3,2,1,0:T(8,128)} fusion(f32[18,8,96,128]{3,2,1,0:T(8,128)} %constant_dynamic-update-slice_fusion.2, f32[16,8,96,128]{3,2,1,0:T(8,128)} %param.6), kind=kLoop, calls=%fused_computation.123 | loop fusion | bytes 12582912
  36.8 25.3 %multiply_add_fusion.5 = f32[16,8,96,128]{3,2,1,0:T(8,128)} fusion(f32[16,8,96,128]{3,2,1,0:T(8,128)} %param.6, f32[16,8,96,128]{3,2,1,0:T(8,128)S(1)} %bitcast.10, f32[16,8,1,128]{3,2,1,0:T(1,128)S(1)} %collective-permute-done.4, f32[18,1,96,128]{3,2,1,0:T(8,128)S(1)} %pad.74, f32[18,8,96,128]{3,2,1,0:T(8,128)} %constant_dynamic-update-slice_fusion, ...), kind=kLoop, calls=%fused_computation.121 | loop fusion | flops 53477376 | bytes 41222144 | tf_op jit(solution)/shard_map/add | solution.py:60
  63.6 4.0 %collective-permute-start.8 = (f32[16,1,96,128]{3,2,1,0:T(8,128)S(1)}, f32[16,1,96,128]{3,2,1,0:T(8,128)S(1)}, u32[]{:S(2)}, u32[]{:S(2)}) collective-permute-start(f32[16,1,96,128]{3,2,1,0:T(8,128)S(1)} %get-tuple-element.69), channel_id=1, source_target_pairs={{2,0},{4,2},{6,4},{3,1},{5,3},{7,5},{10,8},{12,10},{14,12},{11,9},... | collective-permute-start | bytes 2359304 | tf_op jit(solution)/shard_map/ppermute | solution.py:18
  78.6 5.3 %collective-permute-done.8 = f32[16,1,96,128]{3,2,1,0:T(8,128)S(1)} collective-permute-done((f32[16,1,96,128]{3,2,1,0:T(8,128)S(1)}, f32[16,1,96,128]{3,2,1,0:T(8,128)S(1)}, u32[]{:S(2)}, u32[]{:S(2)}) %collective-permute-start.8) | collective-permute-done | bytes 786464 | tf_op jit(solution)/shard_map/ppermute | solution.py:18
  88.2 23.9 %multiply_add_fusion.4 = f32[16,8,96,128]{3,2,1,0:T(8,128)} fusion(f32[16,8,96,128]{3,2,1,0:T(8,128)} %multiply_add_fusion.5, f32[16,8,96,128]{3,2,1,0:T(8,128)S(1)} %bitcast.10, f32[16,8,1,128]{3,2,1,0:T(1,128)S(1)} %collective-permute-done.10, f32[18,1,96,128]{3,2,1,0:T(8,128)S(1)} %pad.78, f32[1,8,96,128]{3,2,1,0:T(8,128)} %collective-permute-done.6, ...), kind=kLoop, calls=%fused_computation.120 | loop fusion | flops 66060288 | bytes 34144256 | tf_op jit(solution)/shard_map/add | solution.py:60
  120.8 3.7 %collective-permute-start.13 = (f32[1,8,96,128]{3,2,1,0:T(8,128)S(1)}, f32[1,8,96,128]{3,2,1,0:T(8,128)}, u32[]{:S(2)}, u32[]{:S(2)}) collective-permute-start(f32[1,8,96,128]{3,2,1,0:T(8,128)S(1)} %get-tuple-element.64), channel_id=1, source_target_pairs={{0,8},{8,16},{16,24},{24,32},{32,40},{40,48},{48,56},{56,64},{64,7... | collective-permute-start | bytes 1179656 | tf_op jit(solution)/shard_map/ppermute | solution.py:17
  127.1 6.0 %collective-permute-done.14 = f32[16,1,96,128]{3,2,1,0:T(8,128)S(1)} collective-permute-done((f32[16,1,96,128]{3,2,1,0:T(8,128)S(1)}, f32[16,1,96,128]{3,2,1,0:T(8,128)S(1)}, u32[]{:S(2)}, u32[]{:S(2)}) %collective-permute-start.14) | collective-permute-done | bytes 786464 | tf_op jit(solution)/shard_map/ppermute | solution.py:18
  137.5 23.1 %multiply_add_fusion.3 = f32[16,8,96,128]{3,2,1,0:T(8,128)} fusion(f32[16,8,96,128]{3,2,1,0:T(8,128)} %multiply_add_fusion.4, f32[16,8,96,128]{3,2,1,0:T(8,128)S(1)} %bitcast.10, f32[16,8,1,128]{3,2,1,0:T(1,128)S(1)} %collective-permute-done.16, f32[18,1,96,128]{3,2,1,0:T(8,128)S(1)} %pad.82, f32[1,8,96,128]{3,2,1,0:T(8,128)} %collective-permute-done.12, ...), kind=kLoop, calls=%fused_computation.119 | loop fusion | flops 66060288 | bytes 34144256 | tf_op jit(solution)/shard_map/add | solution.py:60
  169.5 3.5 collective-permute-start.19
  175.6 6.0 %collective-permute-done.20 = f32[16,1,96,128]{3,2,1,0:T(8,128)S(1)} collective-permute-done((f32[16,1,96,128]{3,2,1,0:T(8,128)S(1)}, f32[16,1,96,128]{3,2,1,0:T(8,128)S(1)}, u32[]{:S(2)}, u32[]{:S(2)}) %collective-permute-start.20) | collective-permute-done | bytes 786464 | tf_op jit(solution)/shard_map/ppermute | solution.py:18
  185.9 23.9 %multiply_add_fusion.2 = f32[16,8,96,128]{3,2,1,0:T(8,128)} fusion(f32[16,8,96,128]{3,2,1,0:T(8,128)} %multiply_add_fusion.3, f32[16,8,96,128]{3,2,1,0:T(8,128)S(1)} %bitcast.10, f32[16,8,1,128]{3,2,1,0:T(1,128)S(1)} %collective-permute-done.22, f32[18,1,96,128]{3,2,1,0:T(8,128)S(1)} %pad.86, f32[1,8,96,128]{3,2,1,0:T(8,128)} %collective-permute-done.18, ...), kind=kLoop, calls=%fused_computation.118 | loop fusion | flops 66060288 | bytes 34144256 | tf_op jit(solution)/shard_map/add | solution.py:60
  219.0 3.5 collective-permute-start.25
  225.1 5.8 %collective-permute-done.26 = f32[16,1,96,128]{3,2,1,0:T(8,128)S(1)} collective-permute-done((f32[16,1,96,128]{3,2,1,0:T(8,128)S(1)}, f32[16,1,96,128]{3,2,1,0:T(8,128)S(1)}, u32[]{:S(2)}, u32[]{:S(2)}) %collective-permute-start.26) | collective-permute-done | bytes 786464 | tf_op jit(solution)/shard_map/ppermute | solution.py:18
  235.2 23.1 %multiply_add_fusion.1 = f32[16,8,96,128]{3,2,1,0:T(8,128)} fusion(f32[16,8,96,128]{3,2,1,0:T(8,128)} %multiply_add_fusion.2, f32[16,8,96,128]{3,2,1,0:T(8,128)S(1)} %bitcast.10, f32[16,8,1,128]{3,2,1,0:T(1,128)S(1)} %collective-permute-done.28, f32[18,1,96,128]{3,2,1,0:T(8,128)S(1)} %pad.90, f32[1,8,96,128]{3,2,1,0:T(8,128)} %collective-permute-done.24, ...), kind=kLoop, calls=%fused_computation.117 | loop fusion | flops 66060288 | bytes 34144256 | tf_op jit(solution)/shard_map/add | solution.py:60
  267.6 3.5 collective-permute-start.31
  273.7 5.6 %collective-permute-done.32 = f32[16,1,96,128]{3,2,1,0:T(8,128)S(1)} collective-permute-done((f32[16,1,96,128]{3,2,1,0:T(8,128)S(1)}, f32[16,1,96,128]{3,2,1,0:T(8,128)S(1)}, u32[]{:S(2)}, u32[]{:S(2)}) %collective-permute-start.32) | collective-permute-done | bytes 786464 | tf_op jit(solution)/shard_map/ppermute | solution.py:18
  283.6 23.9 %multiply_add_fusion = f32[16,8,96,128]{3,2,1,0:T(8,128)} fusion(f32[16,8,96,128]{3,2,1,0:T(8,128)} %multiply_add_fusion.1, f32[16,8,96,128]{3,2,1,0:T(8,128)S(1)} %bitcast.10, f32[16,8,1,128]{3,2,1,0:T(1,128)S(1)} %collective-permute-done.34, f32[18,1,96,128]{3,2,1,0:T(8,128)S(1)} %pad.94, f32[1,8,96,128]{3,2,1,0:T(8,128)} %collective-permute-done.30, ...), kind=kLoop, calls=%fused_computation.116 | loop fusion | flops 66060288 | bytes 34144256 | tf_op jit(solution)/shard_map/add | solution.py:60
  307.6 3.7 fusion.30
  314.9 37.2 %all-gather.3.cloned.1.call-done = f32[64,1,96,128]{3,2,1,0:T(8,128)} async-done(((f32[16,1,96,128]{3,2,1,0:T(8,128)}), f32[64,1,96,128]{3,2,1,0:T(8,128)}) %all-gather.3.cloned.1.call-update) | async-done | bytes 3145744 | tf_op jit(solution)/shard_map/all_gather | solution.py:31
  352.2 4.1 %while.10 = (s32[]{:T(128)}, f32[16,1,96,128]{3,2,1,0:T(8,128)S(1)}, s32[]{:T(128)}, f32[4,16,1,96,128]{4,3,1,2,0:T(8,128)}, s32[]{:T(128)}, /*index=5*/s32[]{:T(128)}, s32[]{:T(128)}) while((s32[]{:T(128)}, f32[16,1,96,128]{3,2,1,0:T(8,128)S(1)}, s32[]{:T(128)}, f32[4,16,1,96,128]{4,3,1,2,0:T(8,128)}, s32[]{:T(128)}, /*index=5*/s32[]{:T(128)}, ...), condition=%wide.region_2.3_spmd, body=%wide.region_1.2_spmd.sunk | while | flops 196613 | bytes 2359411 | solution.py:37
  356.3 6.3 %add_multiply_fusion = f32[16,8,96,128]{3,2,1,0:T(8,128)} fusion(f32[16,8,96,128]{3,2,1,0:T(8,128)} %copy-done, f32[16,96,128]{2,1,0:T(8,128)S(1)} %bitcast.13), kind=kLoop, calls=%fused_computation.115 | loop fusion | flops 3145728 | bytes 13369344 | tf_op jit(solution)/shard_map/div | solution.py:83
  (110 shorter events, 99.5 us)
Async XLA Ops:
  7.2 345.0 %all-gather.3.cloned.1.call-start = ((), (), s32[]{:S(2)}) async-start(), calls=%async_computation | async-start | bytes 3932160 | tf_op jit(solution)/shard_map/all_gather | solution.py:31
  8.4 16.4 %collective-permute-start.1 = (f32[1,8,96,128]{3,2,1,0:T(8,128)S(1)}, f32[1,8,96,128]{3,2,1,0:T(8,128)S(1)}, u32[]{:S(2)}, u32[]{:S(2)}) collective-permute-start(f32[1,8,96,128]{3,2,1,0:T(8,128)S(1)} %get-tuple-element.77), channel_id=1, source_target_pairs={{0,8},{8,16},{16,24},{24,32},{32,40},{40,48},{48,56},{56,64},{64,7... | collective-permute-start | bytes 1179656 | tf_op jit(solution)/shard_map/ppermute | solution.py:17
  13.3 22.7 %collective-permute-start.2 = (f32[16,1,96,128]{3,2,1,0:T(8,128)S(1)}, f32[16,1,96,128]{3,2,1,0:T(8,128)S(1)}, u32[]{:S(2)}, u32[]{:S(2)}) collective-permute-start(f32[16,1,96,128]{3,2,1,0:T(8,128)S(1)} %get-tuple-element.75), channel_id=1, source_target_pairs={{2,0},{4,2},{6,4},{3,1},{5,3},{7,5},{10,8},{12,10},{14,12},{11,9},... | collective-permute-start | bytes 2359304 | tf_op jit(solution)/shard_map/ppermute | solution.py:18
  16.0 20.6 %collective-permute-start.3 = (f32[16,1,96,128]{3,2,1,0:T(8,128)S(1)}, f32[16,1,96,128]{3,2,1,0:T(8,128)S(1)}, u32[]{:S(2)}, u32[]{:S(2)}) collective-permute-start(f32[16,1,96,128]{3,2,1,0:T(8,128)S(1)} %get-tuple-element.74), channel_id=1, source_target_pairs={{0,2},{2,4},{4,6},{1,3},{3,5},{5,7},{8,10},{10,12},{12,14},{9,11},... | collective-permute-start | bytes 2359304 | tf_op jit(solution)/shard_map/ppermute | solution.py:17
  17.3 17.9 %collective-permute-start = (f32[1,8,96,128]{3,2,1,0:T(8,128)S(1)}, f32[1,8,96,128]{3,2,1,0:T(8,128)S(1)}, u32[]{:S(2)}, u32[]{:S(2)}) collective-permute-start(f32[1,8,96,128]{3,2,1,0:T(8,128)S(1)} %get-tuple-element.76), channel_id=1, source_target_pairs={{8,0},{16,8},{24,16},{32,24},{40,32},{48,40},{56,48},{64,56},{72,6... | collective-permute-start | bytes 1179656 | tf_op jit(solution)/shard_map/ppermute | solution.py:18
  63.6 20.3 %collective-permute-start.8 = (f32[16,1,96,128]{3,2,1,0:T(8,128)S(1)}, f32[16,1,96,128]{3,2,1,0:T(8,128)S(1)}, u32[]{:S(2)}, u32[]{:S(2)}) collective-permute-start(f32[16,1,96,128]{3,2,1,0:T(8,128)S(1)} %get-tuple-element.69), channel_id=1, source_target_pairs={{2,0},{4,2},{6,4},{3,1},{5,3},{7,5},{10,8},{12,10},{14,12},{11,9},... | collective-permute-start | bytes 2359304 | tf_op jit(solution)/shard_map/ppermute | solution.py:18
  67.6 20.4 %collective-permute-start.9 = (f32[16,1,96,128]{3,2,1,0:T(8,128)S(1)}, f32[16,1,96,128]{3,2,1,0:T(8,128)S(1)}, u32[]{:S(2)}, u32[]{:S(2)}) collective-permute-start(f32[16,1,96,128]{3,2,1,0:T(8,128)S(1)} %get-tuple-element.68), channel_id=1, source_target_pairs={{0,2},{2,4},{4,6},{1,3},{3,5},{5,7},{8,10},{10,12},{12,14},{9,11},... | collective-permute-start | bytes 2359304 | tf_op jit(solution)/shard_map/ppermute | solution.py:17
  70.1 18.1 %collective-permute-start.6 = (f32[1,8,96,128]{3,2,1,0:T(8,128)S(1)}, f32[1,8,96,128]{3,2,1,0:T(8,128)}, u32[]{:S(2)}, u32[]{:S(2)}) collective-permute-start(f32[1,8,96,128]{3,2,1,0:T(8,128)S(1)} %get-tuple-element.71), channel_id=1, source_target_pairs={{8,0},{16,8},{24,16},{32,24},{40,32},{48,40},{56,48},{64,56},{72,6... | collective-permute-start | bytes 1179656 | tf_op jit(solution)/shard_map/ppermute | solution.py:18
  113.6 19.6 %collective-permute-start.14 = (f32[16,1,96,128]{3,2,1,0:T(8,128)S(1)}, f32[16,1,96,128]{3,2,1,0:T(8,128)S(1)}, u32[]{:S(2)}, u32[]{:S(2)}) collective-permute-start(f32[16,1,96,128]{3,2,1,0:T(8,128)S(1)} %get-tuple-element.63), channel_id=1, source_target_pairs={{2,0},{4,2},{6,4},{3,1},{5,3},{7,5},{10,8},{12,10},{14,12},{11,9},... | collective-permute-start | bytes 2359304 | tf_op jit(solution)/shard_map/ppermute | solution.py:18
  116.2 21.2 %collective-permute-start.15 = (f32[16,1,96,128]{3,2,1,0:T(8,128)S(1)}, f32[16,1,96,128]{3,2,1,0:T(8,128)S(1)}, u32[]{:S(2)}, u32[]{:S(2)}) collective-permute-start(f32[16,1,96,128]{3,2,1,0:T(8,128)S(1)} %get-tuple-element.62), channel_id=1, source_target_pairs={{0,2},{2,4},{4,6},{1,3},{3,5},{5,7},{8,10},{10,12},{12,14},{9,11},... | collective-permute-start | bytes 2359304 | tf_op jit(solution)/shard_map/ppermute | solution.py:17
  118.7 18.8 %collective-permute-start.12 = (f32[1,8,96,128]{3,2,1,0:T(8,128)S(1)}, f32[1,8,96,128]{3,2,1,0:T(8,128)}, u32[]{:S(2)}, u32[]{:S(2)}) collective-permute-start(f32[1,8,96,128]{3,2,1,0:T(8,128)S(1)} %get-tuple-element.65), channel_id=1, source_target_pairs={{8,0},{16,8},{24,16},{32,24},{40,32},{48,40},{56,48},{64,56},{72,6... | collective-permute-start | bytes 1179656 | tf_op jit(solution)/shard_map/ppermute | solution.py:18
  120.8 16.6 %collective-permute-start.13 = (f32[1,8,96,128]{3,2,1,0:T(8,128)S(1)}, f32[1,8,96,128]{3,2,1,0:T(8,128)}, u32[]{:S(2)}, u32[]{:S(2)}) collective-permute-start(f32[1,8,96,128]{3,2,1,0:T(8,128)S(1)} %get-tuple-element.64), channel_id=1, source_target_pairs={{0,8},{8,16},{16,24},{24,32},{32,40},{40,48},{48,56},{56,64},{64,7... | collective-permute-start | bytes 1179656 | tf_op jit(solution)/shard_map/ppermute | solution.py:17
  162.0 19.6 %collective-permute-start.20 = (f32[16,1,96,128]{3,2,1,0:T(8,128)S(1)}, f32[16,1,96,128]{3,2,1,0:T(8,128)S(1)}, u32[]{:S(2)}, u32[]{:S(2)}) collective-permute-start(f32[16,1,96,128]{3,2,1,0:T(8,128)S(1)} %get-tuple-element.57), channel_id=1, source_target_pairs={{2,0},{4,2},{6,4},{3,1},{5,3},{7,5},{10,8},{12,10},{14,12},{11,9},... | collective-permute-start | bytes 2359304 | tf_op jit(solution)/shard_map/ppermute | solution.py:18
  164.6 21.2 %collective-permute-start.21 = (f32[16,1,96,128]{3,2,1,0:T(8,128)S(1)}, f32[16,1,96,128]{3,2,1,0:T(8,128)S(1)}, u32[]{:S(2)}, u32[]{:S(2)}) collective-permute-start(f32[16,1,96,128]{3,2,1,0:T(8,128)S(1)} %get-tuple-element.56), channel_id=1, source_target_pairs={{0,2},{2,4},{4,6},{1,3},{3,5},{5,7},{8,10},{10,12},{12,14},{9,11},... | collective-permute-start | bytes 2359304 | tf_op jit(solution)/shard_map/ppermute | solution.py:17
  167.1 18.8 %collective-permute-start.18 = (f32[1,8,96,128]{3,2,1,0:T(8,128)S(1)}, f32[1,8,96,128]{3,2,1,0:T(8,128)}, u32[]{:S(2)}, u32[]{:S(2)}) collective-permute-start(f32[1,8,96,128]{3,2,1,0:T(8,128)S(1)} %get-tuple-element.59), channel_id=1, source_target_pairs={{8,0},{16,8},{24,16},{32,24},{40,32},{48,40},{56,48},{64,56},{72,6... | collective-permute-start | bytes 1179656 | tf_op jit(solution)/shard_map/ppermute | solution.py:18
  169.5 16.4 %collective-permute-start.19 = (f32[1,8,96,128]{3,2,1,0:T(8,128)S(1)}, f32[1,8,96,128]{3,2,1,0:T(8,128)}, u32[]{:S(2)}, u32[]{:S(2)}) collective-permute-start(f32[1,8,96,128]{3,2,1,0:T(8,128)S(1)} %get-tuple-element.58), channel_id=1, source_target_pairs={{0,8},{8,16},{16,24},{24,32},{32,40},{40,48},{48,56},{56,64},{64,7... | collective-permute-start | bytes 1179656 | tf_op jit(solution)/shard_map/ppermute | solution.py:17
  211.3 19.6 %collective-permute-start.26 = (f32[16,1,96,128]{3,2,1,0:T(8,128)S(1)}, f32[16,1,96,128]{3,2,1,0:T(8,128)S(1)}, u32[]{:S(2)}, u32[]{:S(2)}) collective-permute-start(f32[16,1,96,128]{3,2,1,0:T(8,128)S(1)} %get-tuple-element.51), channel_id=1, source_target_pairs={{2,0},{4,2},{6,4},{3,1},{5,3},{7,5},{10,8},{12,10},{14,12},{11,9},... | collective-permute-start | bytes 2359304 | tf_op jit(solution)/shard_map/ppermute | solution.py:18
  214.1 20.9 %collective-permute-start.27 = (f32[16,1,96,128]{3,2,1,0:T(8,128)S(1)}, f32[16,1,96,128]{3,2,1,0:T(8,128)S(1)}, u32[]{:S(2)}, u32[]{:S(2)}) collective-permute-start(f32[16,1,96,128]{3,2,1,0:T(8,128)S(1)} %get-tuple-element.50), channel_id=1, source_target_pairs={{0,2},{2,4},{4,6},{1,3},{3,5},{5,7},{8,10},{10,12},{12,14},{9,11},... | collective-permute-start | bytes 2359304 | tf_op jit(solution)/shard_map/ppermute | solution.py:17
  216.6 18.6 %collective-permute-start.24 = (f32[1,8,96,128]{3,2,1,0:T(8,128)S(1)}, f32[1,8,96,128]{3,2,1,0:T(8,128)}, u32[]{:S(2)}, u32[]{:S(2)}) collective-permute-start(f32[1,8,96,128]{3,2,1,0:T(8,128)S(1)} %get-tuple-element.53), channel_id=1, source_target_pairs={{8,0},{16,8},{24,16},{32,24},{40,32},{48,40},{56,48},{64,56},{72,6... | collective-permute-start | bytes 1179656 | tf_op jit(solution)/shard_map/ppermute | solution.py:18
  219.0 16.2 %collective-permute-start.25 = (f32[1,8,96,128]{3,2,1,0:T(8,128)S(1)}, f32[1,8,96,128]{3,2,1,0:T(8,128)}, u32[]{:S(2)}, u32[]{:S(2)}) collective-permute-start(f32[1,8,96,128]{3,2,1,0:T(8,128)S(1)} %get-tuple-element.52), channel_id=1, source_target_pairs={{0,8},{8,16},{16,24},{24,32},{32,40},{40,48},{48,56},{56,64},{64,7... | collective-permute-start | bytes 1179656 | tf_op jit(solution)/shard_map/ppermute | solution.py:17
  259.8 19.6 %collective-permute-start.32 = (f32[16,1,96,128]{3,2,1,0:T(8,128)S(1)}, f32[16,1,96,128]{3,2,1,0:T(8,128)S(1)}, u32[]{:S(2)}, u32[]{:S(2)}) collective-permute-start(f32[16,1,96,128]{3,2,1,0:T(8,128)S(1)} %get-tuple-element.45), channel_id=1, source_target_pairs={{2,0},{4,2},{6,4},{3,1},{5,3},{7,5},{10,8},{12,10},{14,12},{11,9},... | collective-permute-start | bytes 2359304 | tf_op jit(solution)/shard_map/ppermute | solution.py:18
  262.8 20.7 %collective-permute-start.33 = (f32[16,1,96,128]{3,2,1,0:T(8,128)S(1)}, f32[16,1,96,128]{3,2,1,0:T(8,128)S(1)}, u32[]{:S(2)}, u32[]{:S(2)}) collective-permute-start(f32[16,1,96,128]{3,2,1,0:T(8,128)S(1)} %get-tuple-element.44), channel_id=1, source_target_pairs={{0,2},{2,4},{4,6},{1,3},{3,5},{5,7},{8,10},{10,12},{12,14},{9,11},... | collective-permute-start | bytes 2359304 | tf_op jit(solution)/shard_map/ppermute | solution.py:17
  265.2 18.4 %collective-permute-start.30 = (f32[1,8,96,128]{3,2,1,0:T(8,128)S(1)}, f32[1,8,96,128]{3,2,1,0:T(8,128)}, u32[]{:S(2)}, u32[]{:S(2)}) collective-permute-start(f32[1,8,96,128]{3,2,1,0:T(8,128)S(1)} %get-tuple-element.47), channel_id=1, source_target_pairs={{8,0},{16,8},{24,16},{32,24},{40,32},{48,40},{56,48},{64,56},{72,6... | collective-permute-start | bytes 1179656 | tf_op jit(solution)/shard_map/ppermute | solution.py:18
  267.6 16.0 %collective-permute-start.31 = (f32[1,8,96,128]{3,2,1,0:T(8,128)S(1)}, f32[1,8,96,128]{3,2,1,0:T(8,128)}, u32[]{:S(2)}, u32[]{:S(2)}) collective-permute-start(f32[1,8,96,128]{3,2,1,0:T(8,128)S(1)} %get-tuple-element.46), channel_id=1, source_target_pairs={{0,8},{8,16},{16,24},{24,32},{32,40},{40,48},{48,56},{56,64},{64,7... | collective-permute-start | bytes 1179656 | tf_op jit(solution)/shard_map/ppermute | solution.py:17
  (18 other events, 161.1 us)
Sparse Core Ops, SparseCore 0:
  315.0 37.0 all-gather.2
where the time goes:
time: 372 us; the launch traced here: 369 us
  other arithmetic  157 us (42%)
  starting transfers between devices  80.3 us (22%)
  waiting for transfers between devices  80.3 us (22%)
  local copies, waits for them, and re-layouts  36.7 us (10%)
  between operations  14.8 us (4%)
    add x6, other arithmetic, single_update(): middle - scaled_wind_north * slopes[0] - scaled_wind_east * slopes[1]  143 us
    ppermute x18, starting transfers between devices, padded(): lax.ppermute(leading, axis, [(b, a) for a, b in up])  42.2 us
    ppermute x18, starting transfers between devices, padded(): lax.ppermute(last, axis, up)  38.1 us
    all_gather x1, waiting for transfers between devices, entering(): gathered = lax.all_gather(part, axis)  37.2 us
    ppermute x18, waiting for transfers between devices, padded(): lax.ppermute(leading, axis, [(b, a) for a, b in up])  28.9 us
    slice x17, local copies, waits for them, and re-layouts, padded(): last = lax.slice_in_dim(x, length - width, length, axis=dim)  22.7 us
    ppermute x18, waiting for transfers between devices, padded(): lax.ppermute(last, axis, up)  14.2 us
    unnamed x12, local copies, waits for them, and re-layouts  10.1 us
  transfers between devices with their start and end apart: 37, of which 12 were waited for; matrix products, arithmetic and copies ran while one was open for 7% of the time, Pallas kernels for 0%

commit v1 on v0

v1 whole, which is shorter than its diff:
```python
import functools

import jax
import jax.numpy as jnp
from jax import lax
from jax.experimental import pallas as pl
from jax.experimental.pallas import tpu as pltpu
from jax.sharding import PartitionSpec as P

STEPS = 6
PAD = 8
MESH = pl.DeviceIdType.MESH


def row_at(k, rows):
    odd = k % 2
    return (1 - odd) * (k // 2) + odd * (rows - 1 - k // 2)


def kernel(
    sizes,
    heat,
    north,
    east,
    up,
    acc,
    end,
    field,
    wind,
    carry,
    onward,
    edge_out,
    edge_in,
    load_sem,
    lon_send,
    lon_recv,
    lat_send,
    lat_recv,
    lev_send,
    lev_recv,
    carry_send,
    carry_recv,
):
    lats, lons, levs = sizes
    rows, cols, deep, members = heat.shape
    lat, lon, lev = (lax.axis_index(name) for name in ("lat", "lon", "lev"))
    body = pl.ds(PAD, deep)

    def remote(src, dst, send, recv, axis, to):
        return pltpu.make_async_remote_copy(
            src_ref=src,
            dst_ref=dst,
            send_sem=send,
            recv_sem=recv,
            device_id={axis: to},
            device_id_type=MESH,
        )

    def lon_copy(slot, y, side, src=None):
        x = (0, cols - 1)[side]
        src = field.at[slot, y + 1, x + 1, body] if src is None else src.at[y, x]
        dst = field.at[slot, y + 1, (cols + 1, 0)[side], body]
        to = lon + (-1, 1)[side]
        return remote(
            src, dst, lon_send.at[side, slot, y], lon_recv.at[side, slot, y], "lon", to
        )

    def lat_copy(slot, side, src=None):
        y = (0, rows - 1)[side]
        src = field.at[slot, y + 1, pl.ds(1, cols), body] if src is None else src.at[y]
        dst = field.at[slot, (rows + 1, 0)[side], pl.ds(1, cols), body]
        to = lat + (-1, 1)[side]
        return remote(
            src, dst, lat_send.at[side, slot], lat_recv.at[side, slot], "lat", to
        )

    def lev_copy(slot, y):
        return remote(
            edge_out.at[slot, y],
            edge_in.at[slot, y],
            lev_send.at[slot, y],
            lev_recv.at[slot, y],
            "lev",
            1 - lev,
        )

    def carry_copy(y):
        return remote(
            onward.at[y], carry.at[y], carry_send.at[y], carry_recv.at[y], "lon", lon + 1
        )

    lon_has = (lon > 0, lon < lons - 1)
    lat_has = (lat > 0, lat < lats - 1)

    def load_heat(y):
        return pltpu.make_async_copy(
            heat.at[y], field.at[0, y + 1, pl.ds(1, cols), body], load_sem.at[3, y]
        )

    def load_wind(d, y):
        return pltpu.make_async_copy(
            (north, east, up)[d].at[y], wind.at[d, y], load_sem.at[d, y]
        )

    barrier = pltpu.get_barrier_semaphore()

    def greet(axis, to):
        pl.semaphore_signal(
            barrier, inc=1, device_id={axis: to}, device_id_type=MESH
        )

    for side in (0, 1):
        pl.when(lon_has[side])(lambda: greet("lon", lon + (-1, 1)[side]))
        pl.when(lat_has[side])(lambda: greet("lat", lat + (-1, 1)[side]))
    greet("lev", 1 - lev)

    def start_heat(k, _):
        load_heat(row_at(k, rows)).start()
        return 0

    def start_wind(k, _):
        for d in range(3):
            load_wind(d, row_at(k, rows)).start()
        return 0

    lax.fori_loop(0, rows, start_heat, 0)
    lax.fori_loop(0, rows, start_wind, 0)

    peers = 1 + sum(has.astype(jnp.int32) for has in (*lon_has, *lat_has))
    pl.semaphore_wait(barrier, peers)

    for side in (0, 1):
        pl.when(lat_has[side])(lambda: lat_copy(0, side, heat).start())

    def start_lon(k, _):
        y = row_at(k, rows)
        for side in (0, 1):
            pl.when(lon_has[side])(lambda: lon_copy(0, y, side, heat).start())
        return 0

    lax.fori_loop(0, rows, start_lon, 0)

    def clear_row(y, _):
        for slot in (0, 1):
            field[slot, y + 1, pl.ds(1, cols), pl.ds(0, PAD), :] = jnp.zeros(
                (cols, PAD, members), jnp.float32
            )
            field[slot, y + 1, pl.ds(1, cols), pl.ds(PAD + deep, PAD), :] = jnp.zeros(
                (cols, PAD, members), jnp.float32
            )
            for side in (0, 1):

                @pl.when(jnp.logical_not(lon_has[side]))
                def _():
                    field[slot, y + 1, (0, cols + 1)[side], body, :] = jnp.zeros(
                        (deep, members), jnp.float32
                    )

        return 0

    lax.fori_loop(0, rows, clear_row, 0)

    def clear_lat(x, _):
        for slot in (0, 1):
            for side in (0, 1):

                @pl.when(jnp.logical_not(lat_has[side]))
                def _():
                    field[slot, (0, rows + 1)[side], x + 1, body, :] = jnp.zeros(
                        (deep, members), jnp.float32
                    )

        return 0

    lax.fori_loop(0, cols, clear_lat, 0)

    edge_from = PAD + (1 - lev) * (deep - 1)
    edge_to = PAD - 1 + (1 - lev) * (deep + 1)

    def first_edges(k, _):
        y = row_at(k, rows)
        load_heat(y).wait()

        def one(x, _):
            edge_out[0, y, pl.ds(x, 1), :] = field[
                0, y + 1, x + 1, pl.ds(edge_from, 1), :
            ]
            return 0

        lax.fori_loop(0, cols, one, 0)
        lev_copy(0, y).start()
        return 0

    lax.fori_loop(0, rows, first_edges, 0)

    def updated(slot, y, x):
        field[slot, y + 1, x + 1, pl.ds(edge_to, 1), :] = edge_in[
            slot, y, pl.ds(x, 1), :
        ]
        middle = field[slot, y + 1, x + 1, body, :]
        lower = (
            field[slot, y, x + 1, body, :],
            field[slot, y + 1, x, body, :],
            field[slot, y + 1, x + 1, pl.ds(PAD - 1, deep), :],
        )
        upper = (
            field[slot, y + 2, x + 1, body, :],
            field[slot, y + 1, x + 2, body, :],
            field[slot, y + 1, x + 1, pl.ds(PAD + 1, deep), :],
        )
        spread = (
            lower[0] + upper[0] + lower[1] + upper[1] + lower[2] + upper[2]
        ) - 6.0 * middle
        value = middle + 0.05 * spread
        for d in range(3):
            value = value - wind[d, y, x, :, :] * (upper[d] - lower[d])
        return value

    def arrivals(slot, y):
        for side in (0, 1):
            pl.when(lon_has[side])(lambda: lon_copy(slot, y, 1 - side).wait_recv())
            pl.when(jnp.logical_and(lat_has[side], y == (0, rows - 1)[side]))(
                lambda: lat_copy(slot, 1 - side).wait_recv()
            )
        lev_copy(slot, y).wait_recv()

    def departures(slot, y):
        for side in (0, 1):
            pl.when(lon_has[side])(lambda: lon_copy(slot, y, side).wait_send())
            pl.when(jnp.logical_and(lat_has[side], y == (0, rows - 1)[side]))(
                lambda: lat_copy(slot, side).wait_send()
            )
        lev_copy(slot, y).wait_send()

    def step(t, _):
        now = t % 2
        later = 1 - now

        def one_row(k, _):
            y = row_at(k, rows)

            @pl.when(t == 0)
            def _():
                for d in range(3):
                    load_wind(d, y).wait()

            arrivals(now, y)
            pl.when(t > 0)(lambda: departures(later, y))

            def one(x, _):
                field[later, y + 1, x + 1, body, :] = updated(now, y, x)
                edge_out[later, y, pl.ds(x, 1), :] = field[
                    later, y + 1, x + 1, pl.ds(edge_from, 1), :
                ]
                return 0

            lax.fori_loop(0, cols, one, 0)
            for side in (0, 1):
                pl.when(lon_has[side])(lambda: lon_copy(later, y, side).start())
                pl.when(jnp.logical_and(lat_has[side], y == (0, rows - 1)[side]))(
                    lambda: lat_copy(later, side).start()
                )
            lev_copy(later, y).start()
            return 0

        lax.fori_loop(0, rows, one_row, 0)
        return 0

    lax.fori_loop(0, STEPS - 1, step, 0)

    last = (STEPS - 1) % 2

    def last_row(k, _):
        y = row_at(k, rows)
        arrivals(last, y)
        departures(1 - last, y)

        def one(x, total):
            value = updated(last, y, x)
            end[y, x, :, :] = value
            total = total + value
            acc[y, x, :, :] = total
            return total

        total = lax.fori_loop(
            0, cols, one, jnp.zeros((deep, members), jnp.float32)
        )

        @pl.when(lon == 0)
        def _():
            onward[y, :, :] = total
            carry_copy(y).start()

        departures(last, y)
        return 0

    lax.fori_loop(0, rows, last_row, 0)

    scale = 1.0 / (cols * lons)

    def finish(k, _):
        y = row_at(k, rows)

        @pl.when(lon > 0)
        def _():
            carry_copy(y).wait_recv()

            @pl.when(lon < lons - 1)
            def _():
                onward[y, :, :] = carry[y, :, :] + acc[y, cols - 1, :, :]
                carry_copy(y).start()

        @pl.when(lon == 0)
        def _():
            carry[y, :, :] = jnp.zeros((deep, members), jnp.float32)

        before = carry[y, :, :]

        def one(x, _):
            acc[y, x, :, :] = (acc[y, x, :, :] + before) * scale
            return 0

        lax.fori_loop(0, cols, one, 0)
        return 0

    lax.fori_loop(0, rows, finish, 0)

    @pl.when(lon < lons - 1)
    def _():
        def drain(k, _):
            carry_copy(row_at(k, rows)).wait_send()
            return 0

        lax.fori_loop(0, rows, drain, 0)


def per_device(sizes, heat, north, east, up):
    rows, cols, deep, members = heat.shape
    shape = jax.ShapeDtypeStruct(heat.shape, heat.dtype)
    f32 = jnp.float32
    dma = pltpu.SemaphoreType.DMA
    return pl.pallas_call(
        functools.partial(kernel, sizes),
        out_shape=(shape, shape),
        in_specs=[pl.BlockSpec(memory_space=pl.ANY)] * 4,
        out_specs=(pl.BlockSpec(memory_space=pltpu.VMEM),) * 2,
        scratch_shapes=[
            pltpu.VMEM((2, rows + 2, cols + 2, deep + 2 * PAD, members), f32),
            pltpu.VMEM((3, rows, cols, deep, members), f32),
            pltpu.VMEM((rows, deep, members), f32),
            pltpu.VMEM((rows, deep, members), f32),
            pltpu.VMEM((2, rows, cols, members), f32),
            pltpu.VMEM((2, rows, cols, members), f32),
            dma((4, rows)),
            dma((2, 2, rows)),
            dma((2, 2, rows)),
            dma((2, 2)),
            dma((2, 2)),
            dma((2, rows)),
            dma((2, rows)),
            dma((rows,)),
            dma((rows,)),
        ],
        compiler_params=pltpu.CompilerParams(
            collective_id=0,
            has_side_effects=True,
            vmem_limit_bytes=40 * 1024 * 1024,
        ),
    )(heat, north, east, up)


def solution(mesh):
    sizes = tuple(mesh.shape[name] for name in ("lat", "lon", "lev"))
    spec = P("lat", "lon", "lev", None)
    return jax.shard_map(
        functools.partial(per_device, sizes),
        mesh=mesh,
        in_specs=(spec,) * 4,
        out_specs=(spec, spec),
        check_vma=False,
    )
```

time: 372 us -> 136 us (0.37)
  other arithmetic: 157 us -> 0 us
  Pallas kernels: 0 us -> 130 us
  starting transfers between devices: 80.3 us -> 0 us
  waiting for transfers between devices: 80.3 us -> 0 us
  local copies, waits for them, and re-layouts: 36.7 us -> 5.41 us
  between operations: 14.8 us -> 0.64 us
    add x9 -> x0, other arithmetic: 147 us -> none  [the longest x6 143 us: single_update(): middle - scaled_wind_north * slopes[0] - scaled_wind_east * slopes[1]]
    pallas_call x0 -> x1, Pallas kernels: none -> 130 us  [per_device(): pl.pallas_call(functools.partial(kernel, sizes), out_shape=(shape, shape)...]
    ppermute x36 -> x0, starting transfers between devices: 80.3 us -> none  [the longest x18 42.2 us: padded(): lax.ppermute(leading, axis, [(b, a) for a, b in up])]
    ppermute x36 -> x0, waiting for transfers between devices: 43.1 us -> none  [the longest x18 28.9 us: padded(): lax.ppermute(leading, axis, [(b, a) for a, b in up])]
    all_gather x1 -> x0, waiting for transfers between devices: 37.2 us -> none  [entering(): gathered = lax.all_gather(part, axis)]
    slice x19 -> x0, local copies, waits for them, and re-layouts: 24.9 us -> none  [the longest x17 22.7 us: padded(): last = lax.slice_in_dim(x, length - width, length, axis=dim)]
    div x1 -> x0, other arithmetic: 6.26 us -> none  [per_device(): (present_layer + beneath_layer) / (initial_heat.shape[1] * lax.axis_size(...]
    unnamed x12 -> x2, local copies, waits for them, and re-layouts: 10.1 us -> 5.41 us
  transfers between devices with their start and end apart: 37 -> 0, of which waited for: 12 -> 0; matrix products, arithmetic and copies ran while one was open for 7% -> 0% of each run, Pallas kernels for 0% -> 0%
where the time goes in v1:
time: 136 us
  Pallas kernels  130 us (96%)
  local copies, waits for them, and re-layouts  5.41 us (4%)
    pallas_call x1, Pallas kernels, per_device(): pl.pallas_call(functools.partial(kernel, sizes), out_shape=(shape, shape)...  130 us
    unnamed x2, local copies, waits for them, and re-layouts  5.41 us

profile of v1, /device:TPU:120, one launch (start us, length us, event | category | flops | bytes accessed | tf_op | source)
XLA Modules:
  0.0 136.0 jit_solution(15073370879942800521)
XLA Ops:
  0.6 129.9 %shard_map.59 = (f32[16,8,96,128]{3,2,1,0:T(8,128)S(1)}, f32[16,8,96,128]{3,2,1,0:T(8,128)S(1)}) custom-call(f32[16,8,96,128]{3,2,1,0:T(8,128)} %heat.1, f32[16,8,96,128]{3,2,1,0:T(8,128)} %north.1, f32[16,8,96,128]{3,2,1,0:T(8,128)} %east.1, f32[16,8,96,128]{3,2,1,0:T(8,128)} %up.1), custom_call_target="tpu_custom_call" | custom-call | tf_op jit(solution)/shard_map/pallas_call | solution.py:342
  130.6 2.7 %copy.8 = f32[16,8,96,128]{3,2,1,0:T(8,128)} copy(f32[16,8,96,128]{3,2,1,0:T(8,128)S(1)} %get-tuple-element.4) | data formatting | bytes 12582912
  133.3 2.7 %copy.9 = f32[16,8,96,128]{3,2,1,0:T(8,128)} copy(f32[16,8,96,128]{3,2,1,0:T(8,128)S(1)} %get-tuple-element.5) | data formatting | bytes 12582912

commit v2 on v1

--- a/solution.py
+++ b/solution.py
@@ -334,12 +334,27 @@
         lax.fori_loop(0, rows, drain, 0)
 
 
+def store_kernel(acc, end, acc_out, end_out, sem):
+    def both(y):
+        return (
+            pltpu.make_async_copy(end.at[y], end_out.at[y], sem.at[0, y]),
+            pltpu.make_async_copy(acc.at[y], acc_out.at[y], sem.at[1, y]),
+        )
+
+    for y in range(acc.shape[0]):
+        for copy in both(y):
+            copy.start()
+    for y in range(acc.shape[0]):
+        for copy in both(y):
+            copy.wait()
+
+
 def per_device(sizes, heat, north, east, up):
     rows, cols, deep, members = heat.shape
     shape = jax.ShapeDtypeStruct(heat.shape, heat.dtype)
     f32 = jnp.float32
     dma = pltpu.SemaphoreType.DMA
-    return pl.pallas_call(
+    acc, end = pl.pallas_call(
         functools.partial(kernel, sizes),
         out_shape=(shape, shape),
         in_specs=[pl.BlockSpec(memory_space=pl.ANY)] * 4,
@@ -367,6 +382,14 @@
             vmem_limit_bytes=40 * 1024 * 1024,
         ),
     )(heat, north, east, up)
+    return pl.pallas_call(
+        store_kernel,
+        out_shape=(shape, shape),
+        in_specs=[pl.BlockSpec(memory_space=pltpu.VMEM)] * 2,
+        out_specs=(pl.BlockSpec(memory_space=pltpu.HBM),) * 2,
+        scratch_shapes=[dma((2, rows))],
+        compiler_params=pltpu.CompilerParams(vmem_limit_bytes=1024 * 1024),
+    )(acc, end)
 
 
 def solution(mesh):

time: 136 us -> 135 us (level)
  local copies, waits for them, and re-layouts: 5.41 us -> 0 us
  Pallas kernels: 130 us -> 135 us
    unnamed x2 -> x0, local copies, waits for them, and re-layouts: 5.41 us -> none
    pallas_call x0 -> x1, Pallas kernels: none -> 4.81 us  [per_device(): pl.pallas_call(store_kernel, out_shape=(shape, shape), in_specs=[pl.Block...]
where the time goes in v2:
time: 135 us
  Pallas kernels  135 us (100%)
    pallas_call x1, Pallas kernels, per_device(): pl.pallas_call(functools.partial(kernel, sizes), out_shape=(shape, shape)...  130 us
    pallas_call x1, Pallas kernels, per_device(): pl.pallas_call(store_kernel, out_shape=(shape, shape), in_specs=[pl.Block...  4.81 us

profile of v2, /device:TPU:120, one launch (start us, length us, event | category | flops | bytes accessed | tf_op | source)
XLA Modules:
  0.0 135.4 jit_solution(16961229707380543922)
XLA Ops:
  0.6 129.9 %shard_map.59 = (f32[16,8,96,128]{3,2,1,0:T(8,128)S(1)}, f32[16,8,96,128]{3,2,1,0:T(8,128)S(1)}) custom-call(f32[16,8,96,128]{3,2,1,0:T(8,128)} %heat.1, f32[16,8,96,128]{3,2,1,0:T(8,128)} %north.1, f32[16,8,96,128]{3,2,1,0:T(8,128)} %east.1, f32[16,8,96,128]{3,2,1,0:T(8,128)} %up.1), custom_call_target="tpu_custom_call" | custom-call | tf_op jit(solution)/shard_map/pallas_call | solution.py:357
  130.6 4.8 %shard_map.60 = (f32[16,8,96,128]{3,2,1,0:T(8,128)}, f32[16,8,96,128]{3,2,1,0:T(8,128)}) custom-call(f32[16,8,96,128]{3,2,1,0:T(8,128)S(1)} %get-tuple-element.4.acc, f32[16,8,96,128]{3,2,1,0:T(8,128)S(1)} %get-tuple-element.5.end), custom_call_target="tpu_custom_call" | custom-call | tf_op jit(solution)/shard_map/pallas_call | solution.py:385

commit v3 on v2

--- a/solution.py
+++ b/solution.py
@@ -27,8 +27,8 @@
     end,
     field,
     wind,
-    carry,
-    onward,
+    from_low,
+    from_high,
     edge_out,
     edge_in,
     load_sem,
@@ -38,8 +38,10 @@
     lat_recv,
     lev_send,
     lev_recv,
-    carry_send,
-    carry_recv,
+    up_send,
+    up_recv,
+    down_send,
+    down_recv,
 ):
     lats, lons, levs = sizes
     rows, cols, deep, members = heat.shape
@@ -84,9 +86,15 @@
             1 - lev,
         )
 
-    def carry_copy(y):
+    def up_copy(y, src):
         return remote(
-            onward.at[y], carry.at[y], carry_send.at[y], carry_recv.at[y], "lon", lon + 1
+            src, from_low.at[y], up_send.at[y], up_recv.at[y], "lon", lon + 1
+        )
+
+    def down_copy(y, src):
+        to = (lon + lons - 1) % lons
+        return remote(
+            src, from_high.at[y], down_send.at[y], down_recv.at[y], "lon", to
         )
 
     lon_has = (lon > 0, lon < lons - 1)
@@ -110,7 +118,7 @@
         )
 
     for side in (0, 1):
-        pl.when(lon_has[side])(lambda: greet("lon", lon + (-1, 1)[side]))
+        greet("lon", (lon + (lons - 1, 1)[side]) % lons)
         pl.when(lat_has[side])(lambda: greet("lat", lat + (-1, 1)[side]))
     greet("lev", 1 - lev)
 
@@ -126,7 +134,7 @@
     lax.fori_loop(0, rows, start_heat, 0)
     lax.fori_loop(0, rows, start_wind, 0)
 
-    peers = 1 + sum(has.astype(jnp.int32) for has in (*lon_has, *lat_has))
+    peers = 3 + sum(has.astype(jnp.int32) for has in lat_has)
     pl.semaphore_wait(barrier, peers)
 
     for side in (0, 1):
@@ -269,9 +277,35 @@
     lax.fori_loop(0, STEPS - 1, step, 0)
 
     last = (STEPS - 1) % 2
+    scale = 1.0 / (cols * lons)
+
+    quarter = rows // 4
+
+    def row_b(j):
+        return row_at(4 * j, rows)
+
+    def row_e(j):
+        return row_at(4 * j + 1, rows)
+
+    def row_a(j):
+        return row_at(4 * j + 2, rows)
+
+    def row_c(j):
+        return row_at(4 * j + 3, rows)
+
+    def own(y):
+        return acc.at[y, cols - 1]
+
+    def each(body_of):
+        def one(j, _):
+            body_of(j)
+            return 0
+
+        lax.fori_loop(0, quarter, one, 0)
 
     def last_row(k, _):
         y = row_at(k, rows)
+        way = k % 4
         arrivals(last, y)
         departures(1 - last, y)
 
@@ -279,59 +313,147 @@
             value = updated(last, y, x)
             end[y, x, :, :] = value
             total = total + value
-            acc[y, x, :, :] = total
+            acc[y, x, :, :] = total * scale
             return total
 
-        total = lax.fori_loop(
-            0, cols, one, jnp.zeros((deep, members), jnp.float32)
-        )
-
-        @pl.when(lon == 0)
-        def _():
-            onward[y, :, :] = total
-            carry_copy(y).start()
-
+        lax.fori_loop(0, cols, one, jnp.zeros((deep, members), jnp.float32))
+
+        def first(place, number):
+            return jnp.logical_and(lon == place, way == number)
+
+        up_first = jnp.logical_or(
+            first(0, 2), jnp.logical_or(first(1, 0), first(2, 3))
+        )
+        down_first = jnp.logical_or(
+            first(0, 0), jnp.logical_or(first(1, 3), first(2, 1))
+        )
+        pl.when(up_first)(lambda: up_copy(y, own(y)).start())
+        pl.when(down_first)(lambda: down_copy(y, own(y)).start())
         departures(last, y)
         return 0
 
     lax.fori_loop(0, rows, last_row, 0)
 
-    scale = 1.0 / (cols * lons)
-
-    def finish(k, _):
-        y = row_at(k, rows)
-
-        @pl.when(lon > 0)
-        def _():
-            carry_copy(y).wait_recv()
-
-            @pl.when(lon < lons - 1)
-            def _():
-                onward[y, :, :] = carry[y, :, :] + acc[y, cols - 1, :, :]
-                carry_copy(y).start()
-
-        @pl.when(lon == 0)
-        def _():
-            carry[y, :, :] = jnp.zeros((deep, members), jnp.float32)
-
-        before = carry[y, :, :]
-
+    def got_low(y):
+        up_copy(y, own(y)).wait_recv()
+        return from_low[y, :, :]
+
+    def got_high(y):
+        down_copy(y, own(y)).wait_recv()
+        return from_high[y, :, :]
+
+    def relay_up(y, value):
+        from_low[y, :, :] = value + acc[y, cols - 1, :, :]
+        up_copy(y, from_low.at[y]).start()
+
+    def relay_down(y, value):
+        from_high[y, :, :] = value + acc[y, cols - 1, :, :]
+        down_copy(y, from_high.at[y]).start()
+
+    def pass_down(y):
+        down_copy(y, own(y)).wait_recv()
+        down_copy(y, from_high.at[y]).start()
+
+    def up_gone(y):
+        up_copy(y, own(y)).wait_send()
+
+    def down_gone(y):
+        down_copy(y, own(y)).wait_send()
+
+    def finish(y, before):
         def one(x, _):
-            acc[y, x, :, :] = (acc[y, x, :, :] + before) * scale
+            acc[y, x, :, :] = acc[y, x, :, :] + before
             return 0
 
         lax.fori_loop(0, cols, one, 0)
-        return 0
-
-    lax.fori_loop(0, rows, finish, 0)
-
-    @pl.when(lon < lons - 1)
+
+    @pl.when(lon == 0)
     def _():
-        def drain(k, _):
-            carry_copy(row_at(k, rows)).wait_send()
-            return 0
-
-        lax.fori_loop(0, rows, drain, 0)
+        each(lambda j: up_copy(row_e(j), own(row_e(j))).start())
+        each(lambda j: up_copy(row_c(j), own(row_c(j))).start())
+        each(lambda j: relay_down(row_c(j), got_high(row_c(j))))
+        each(lambda j: relay_down(row_e(j), got_high(row_e(j))))
+        for row in (row_a, row_e, row_c):
+            each(lambda j: up_gone(row(j)))
+        for row in (row_b, row_c, row_e):
+            each(lambda j: down_gone(row(j)))
+
+    @pl.when(lon == 1)
+    def _():
+        def first(j):
+            y = row_a(j)
+            before = got_low(y)
+            relay_up(y, before)
+            relay_down(row_e(j), got_high(row_e(j)))
+            finish(y, before)
+
+        def second(j):
+            y = row_e(j)
+            before = got_low(y)
+            relay_up(y, before)
+            finish(y, before)
+
+        def third(j):
+            y = row_b(j)
+            up_gone(y)
+            finish(y, got_high(y))
+
+        def fourth(j):
+            y = row_c(j)
+            down_gone(y)
+            finish(y, got_low(y))
+
+        for part in (first, second, third, fourth):
+            each(part)
+        each(lambda j: up_gone(row_a(j)))
+        each(lambda j: up_gone(row_e(j)))
+        each(lambda j: down_gone(row_e(j)))
+
+    @pl.when(lon == 2)
+    def _():
+        def first(j):
+            y = row_b(j)
+            low = got_low(y)
+            relay_up(y, low)
+            pass_down(y)
+            finish(y, low + from_high[y, :, :])
+
+        def second(j):
+            y = row_a(j)
+            before = got_low(y)
+            relay_up(y, before)
+            finish(y, before)
+
+        def third(j):
+            y = row_c(j)
+            up_gone(y)
+            finish(y, got_high(y))
+
+        def fourth(j):
+            y = row_e(j)
+            down_gone(y)
+            finish(y, got_low(y))
+
+        for part in (first, second, third, fourth):
+            each(part)
+        each(lambda j: up_gone(row_b(j)))
+        each(lambda j: up_gone(row_a(j)))
+        each(lambda j: down_gone(row_b(j)))
+
+    @pl.when(lon == 3)
+    def _():
+        each(lambda j: pass_down(row_b(j)))
+        each(lambda j: pass_down(row_c(j)))
+
+        def both(y):
+            finish(y, got_low(y) + from_high[y, :, :])
+
+        each(lambda j: both(row_c(j)))
+        each(lambda j: both(row_b(j)))
+        each(lambda j: finish(row_e(j), got_high(row_e(j))))
+        each(lambda j: finish(row_a(j), got_low(row_a(j))))
+        each(lambda j: down_gone(row_b(j)))
+        each(lambda j: down_gone(row_c(j)))
 
 
 def store_kernel(acc, end, acc_out, end_out, sem):
@@ -375,6 +497,8 @@
             dma((2, rows)),
             dma((rows,)),
             dma((rows,)),
+            dma((rows,)),
+            dma((rows,)),
         ],
         compiler_params=pltpu.CompilerParams(
             collective_id=0,

time: 135 us -> 127 us (0.941)
  Pallas kernels: 135 us -> 126 us
    pallas_call x1, Pallas kernels: 130 us -> 121 us  [per_device(): pl.pallas_call(functools.partial(kernel, sizes), out_shape=(shape, shape)...]
where the time goes in v3:
time: 127 us
  Pallas kernels  126 us (99%)
    pallas_call x1, Pallas kernels, per_device(): pl.pallas_call(functools.partial(kernel, sizes), out_shape=(shape, shape)...  121 us
    pallas_call x1, Pallas kernels, per_device(): pl.pallas_call(store_kernel, out_shape=(shape, shape), in_specs=[pl.Block...  4.81 us

profile of v3, /device:TPU:120, one launch (start us, length us, event | category | flops | bytes accessed | tf_op | source)
XLA Modules:
  0.0 126.7 jit_solution(12072087341149667726)
XLA Ops:
  0.6 121.2 %shard_map.59 = (f32[16,8,96,128]{3,2,1,0:T(8,128)S(1)}, f32[16,8,96,128]{3,2,1,0:T(8,128)S(1)}) custom-call(f32[16,8,96,128]{3,2,1,0:T(8,128)} %heat.1, f32[16,8,96,128]{3,2,1,0:T(8,128)} %north.1, f32[16,8,96,128]{3,2,1,0:T(8,128)} %east.1, f32[16,8,96,128]{3,2,1,0:T(8,128)} %up.1), custom_call_target="tpu_custom_call" | custom-call | tf_op jit(solution)/shard_map/pallas_call | solution.py:479
  121.9 4.8 %shard_map.60 = (f32[16,8,96,128]{3,2,1,0:T(8,128)}, f32[16,8,96,128]{3,2,1,0:T(8,128)}) custom-call(f32[16,8,96,128]{3,2,1,0:T(8,128)S(1)} %get-tuple-element.4.acc, f32[16,8,96,128]{3,2,1,0:T(8,128)S(1)} %get-tuple-element.5.end), custom_call_target="tpu_custom_call" | custom-call | tf_op jit(solution)/shard_map/pallas_call | solution.py:509

commit v4 on v3

v4 whole, which is shorter than its diff:
```python
import functools

import jax
import jax.numpy as jnp
from jax import lax
from jax.experimental import pallas as pl
from jax.experimental.pallas import tpu as pltpu
from jax.sharding import PartitionSpec as P

STEPS = 6
PAD = 8
MESH = pl.DeviceIdType.MESH


def row_at(k, rows):
    odd = k % 2
    return (1 - odd) * (k // 2) + odd * (rows - 1 - k // 2)


def kernel(
    sizes,
    heat,
    north,
    east,
    up,
    acc,
    end,
    field,
    wind,
    from_low,
    from_high,
    edge_out,
    edge_in,
    heat_sem,
    wind_sem,
    lon_send,
    lon_recv,
    lat_send,
    lat_recv,
    lev_send,
    lev_recv,
    sum_send,
):
    lats, lons, levs = sizes
    rows, cols, deep, members = heat.shape
    lat, lon, lev = (lax.axis_index(name) for name in ("lat", "lon", "lev"))
    body = pl.ds(PAD, deep)

    def remote(src, dst, send, recv, axis, to):
        return pltpu.make_async_remote_copy(
            src_ref=src,
            dst_ref=dst,
            send_sem=send,
            recv_sem=recv,
            device_id={axis: to},
            device_id_type=MESH,
        )

    quarter, half = rows // 4, rows // 2

    def lon_copy(slot, k, side):
        y = row_at(k, rows)
        return remote(
            field.at[slot, y + 1, (1, cols)[side], body],
            field.at[slot, y + 1, (cols + 1, 0)[side], body],
            lon_send.at[side, slot, k // quarter],
            lon_recv.at[side, slot, y],
            "lon",
            lon + (-1, 1)[side],
        )

    def lon_gone(slot, part, side):
        some = field.at[slot, pl.ds(1, quarter), 1, body]
        remote(
            some,
            some,
            lon_send.at[side, slot, part],
            lon_recv.at[side, slot, 0],
            "lon",
            lon + (-1, 1)[side],
        ).wait_send()

    def lat_copy(slot, side):
        src = field.at[slot, (1, rows)[side], pl.ds(1, cols), body]
        dst = field.at[slot, (rows + 1, 0)[side], pl.ds(1, cols), body]
        to = lat + (-1, 1)[side]
        return remote(
            src, dst, lat_send.at[side, slot], lat_recv.at[side, slot], "lat", to
        )

    def lev_copy(slot, part):
        some = pl.ds(part * half, half)
        return remote(
            edge_out.at[slot, some],
            edge_in.at[slot, some],
            lev_send.at[slot, part],
            lev_recv.at[slot, part],
            "lev",
            1 - lev,
        )

    spare = STEPS % 2

    def up_copy(y, way, src):
        return remote(
            src,
            from_low.at[y],
            sum_send.at[1, way],
            lon_recv.at[1, spare, y],
            "lon",
            lon + 1,
        )

    def down_copy(y, way, src):
        return remote(
            src,
            from_high.at[y],
            sum_send.at[0, way],
            lon_recv.at[0, spare, y],
            "lon",
            (lon + lons - 1) % lons,
        )

    def sums_gone(side, way):
        some = from_low.at[pl.ds(0, quarter)]
        remote(
            some,
            some,
            sum_send.at[side, way],
            lon_recv.at[side, spare, 0],
            "lon",
            (lon + (lons - 1, 1)[side]) % lons,
        ).wait_send()

    lon_has = (lon > 0, lon < lons - 1)
    lat_has = (lat > 0, lat < lats - 1)

    def load_heat(first, count, part):
        return pltpu.make_async_copy(
            heat.at[pl.ds(first, count)],
            field.at[0, pl.ds(first + 1, count), pl.ds(1, cols), body],
            heat_sem.at[part],
        )

    def load_wind(d):
        return pltpu.make_async_copy(
            (north, east, up)[d], wind.at[d], wind_sem.at[d]
        )

    barrier = pltpu.get_barrier_semaphore()

    def greet(axis, to):
        pl.semaphore_signal(
            barrier, inc=1, device_id={axis: to}, device_id_type=MESH
        )

    for side in (0, 1):
        greet("lon", (lon + (lons - 1, 1)[side]) % lons)
        pl.when(lat_has[side])(lambda: greet("lat", lat + (-1, 1)[side]))
    greet("lev", 1 - lev)

    load_heat(0, quarter, 0).start()
    load_heat(rows - quarter, quarter, 0).start()
    load_heat(quarter, half, 1).start()

    peers = 3 + sum(has.astype(jnp.int32) for has in lat_has)
    pl.semaphore_wait(barrier, peers)

    edge_from = PAD + (1 - lev) * (deep - 1)
    edge_to = PAD - 1 + (1 - lev) * (deep + 1)

    def send_row(slot, k):
        y = row_at(k, rows)
        for side in (0, 1):
            pl.when(lon_has[side])(lambda: lon_copy(slot, k, side).start())
            pl.when(jnp.logical_and(lat_has[side], y == (0, rows - 1)[side]))(
                lambda: lat_copy(slot, side).start()
            )

    def first_row(k, _):
        send_row(0, k)
        return 0

    for part in (0, 1):
        load_heat(0, half, part).wait()
        lax.fori_loop(part * half, (part + 1) * half, first_row, 0)
    for d in range(3):
        load_wind(d).start()

    def first_edges(k, _):
        y = row_at(k, rows)

        def one(x, _):
            edge_out[0, k, pl.ds(x, 1), :] = field[
                0, y + 1, x + 1, pl.ds(edge_from, 1), :
            ]
            return 0

        lax.fori_loop(0, cols, one, 0)
        return 0

    for part in (0, 1):
        lax.fori_loop(part * half, (part + 1) * half, first_edges, 0)
        lev_copy(0, part).start()

    def clear_row(y, _):
        for slot in (0, 1):
            field[slot, y + 1, pl.ds(1, cols), pl.ds(0, PAD), :] = jnp.zeros(
                (cols, PAD, members), jnp.float32
            )
            field[slot, y + 1, pl.ds(1, cols), pl.ds(PAD + deep, PAD), :] = jnp.zeros(
                (cols, PAD, members), jnp.float32
            )
            for side in (0, 1):

                @pl.when(jnp.logical_not(lon_has[side]))
                def _():
                    field[slot, y + 1, (0, cols + 1)[side], body, :] = jnp.zeros(
                        (deep, members), jnp.float32
                    )

        return 0

    lax.fori_loop(0, rows, clear_row, 0)

    def clear_lat(x, _):
        for slot in (0, 1):
            for side in (0, 1):

                @pl.when(jnp.logical_not(lat_has[side]))
                def _():
                    field[slot, (0, rows + 1)[side], x + 1, body, :] = jnp.zeros(
                        (deep, members), jnp.float32
                    )

        return 0

    lax.fori_loop(0, cols, clear_lat, 0)

    def updated(slot, k, y, x):
        field[slot, y + 1, x + 1, pl.ds(edge_to, 1), :] = edge_in[
            slot, k, pl.ds(x, 1), :
        ]
        middle = field[slot, y + 1, x + 1, body, :]
        lower = (
            field[slot, y, x + 1, body, :],
            field[slot, y + 1, x, body, :],
            field[slot, y + 1, x + 1, pl.ds(PAD - 1, deep), :],
        )
        upper = (
            field[slot, y + 2, x + 1, body, :],
            field[slot, y + 1, x + 2, body, :],
            field[slot, y + 1, x + 1, pl.ds(PAD + 1, deep), :],
        )
        spread = (
            lower[0] + upper[0] + lower[1] + upper[1] + lower[2] + upper[2]
        ) - 6.0 * middle
        value = middle + 0.05 * spread
        for d in range(3):
            value = value - wind[d, y, x, :, :] * (upper[d] - lower[d])
        return value

    def arrivals(slot, k):
        y = row_at(k, rows)
        for side in (0, 1):
            pl.when(lon_has[side])(lambda: lon_copy(slot, k, 1 - side).wait_recv())
            pl.when(jnp.logical_and(lat_has[side], y == (0, rows - 1)[side]))(
                lambda: lat_copy(slot, 1 - side).wait_recv()
            )
        pl.when(k % half == 0)(lambda: lev_copy(slot, k // half).wait_recv())

    def departures(slot, k):
        y = row_at(k, rows)
        for side in (0, 1):
            pl.when(jnp.logical_and(lon_has[side], k % quarter == 0))(
                lambda: lon_gone(slot, k // quarter, side)
            )
            pl.when(jnp.logical_and(lat_has[side], y == (0, rows - 1)[side]))(
                lambda: lat_copy(slot, side).wait_send()
            )
        pl.when(k % half == 0)(lambda: lev_copy(slot, k // half).wait_send())

    def step(t, _):
        now = t % 2
        later = 1 - now

        @pl.when(t == 0)
        def _():
            for d in range(3):
                load_wind(d).wait()

        def one_row(k, _):
            y = row_at(k, rows)
            arrivals(now, k)
            pl.when(t > 0)(lambda: departures(later, k))

            def one(x, _):
                field[later, y + 1, x + 1, body, :] = updated(now, k, y, x)
                edge_out[later, k, pl.ds(x, 1), :] = field[
                    later, y + 1, x + 1, pl.ds(edge_from, 1), :
                ]
                return 0

            lax.fori_loop(0, cols, one, 0)
            send_row(later, k)
            pl.when(k % half == half - 1)(lambda: lev_copy(later, k // half).start())
            return 0

        lax.fori_loop(0, rows, one_row, 0)
        return 0

    lax.fori_loop(0, STEPS - 1, step, 0)

    last = (STEPS - 1) % 2
    scale = 1.0 / (cols * lons)

    way_b, way_e, way_a, way_c = range(4)

    def row_b(j):
        return row_at(4 * j, rows)

    def row_e(j):
        return row_at(4 * j + 1, rows)

    def row_a(j):
        return row_at(4 * j + 2, rows)

    def row_c(j):
        return row_at(4 * j + 3, rows)

    def own(y):
        return acc.at[y, cols - 1]

    def each(body_of):
        def one(j, _):
            body_of(j)
            return 0

        lax.fori_loop(0, quarter, one, 0)

    def last_row(k, _):
        y = row_at(k, rows)
        way = k % 4
        arrivals(last, k)
        departures(spare, k)

        def one(x, total):
            value = updated(last, k, y, x)
            end[y, x, :, :] = value
            total = total + value
            acc[y, x, :, :] = total * scale
            return total

        lax.fori_loop(0, cols, one, jnp.zeros((deep, members), jnp.float32))

        def first(place, number):
            return jnp.logical_and(lon == place, way == number)

        up_first = jnp.logical_or(
            first(0, 2), jnp.logical_or(first(1, 0), first(2, 3))
        )
        down_first = jnp.logical_or(
            first(0, 0), jnp.logical_or(first(1, 3), first(2, 1))
        )
        pl.when(up_first)(lambda: up_copy(y, way, own(y)).start())
        pl.when(down_first)(lambda: down_copy(y, way, own(y)).start())
        return 0

    lax.fori_loop(0, rows, last_row, 0)

    def halo_gone(k, _):
        departures(last, k)
        return 0

    lax.fori_loop(0, rows, halo_gone, 0)

    def got_low(y):
        up_copy(y, 0, own(y)).wait_recv()
        return from_low[y, :, :]

    def got_high(y):
        down_copy(y, 0, own(y)).wait_recv()
        return from_high[y, :, :]

    def relay_up(y, way, value):
        from_low[y, :, :] = value + acc[y, cols - 1, :, :]
        up_copy(y, way, from_low.at[y]).start()

    def relay_down(y, way, value):
        from_high[y, :, :] = value + acc[y, cols - 1, :, :]
        down_copy(y, way, from_high.at[y]).start()

    def pass_down(y, way):
        down_copy(y, 0, own(y)).wait_recv()
        down_copy(y, way, from_high.at[y]).start()

    def finish(y, before):
        def one(x, _):
            acc[y, x, :, :] = acc[y, x, :, :] + before
            return 0

        lax.fori_loop(0, cols, one, 0)

    def drain(up, down):
        for way in up:
            sums_gone(1, way)
        for way in down:
            sums_gone(0, way)

    @pl.when(lon == 0)
    def _():
        each(lambda j: up_copy(row_e(j), way_e, own(row_e(j))).start())
        each(lambda j: up_copy(row_c(j), way_c, own(row_c(j))).start())
        each(lambda j: relay_down(row_c(j), way_c, got_high(row_c(j))))
        each(lambda j: relay_down(row_e(j), way_e, got_high(row_e(j))))
        drain((way_a, way_e, way_c), (way_b, way_c, way_e))

    @pl.when(lon == 1)
    def _():
        def first(j):
            y = row_a(j)
            before = got_low(y)
            relay_up(y, way_a, before)
            relay_down(row_e(j), way_e, got_high(row_e(j)))
            finish(y, before)

        def second(j):
            y = row_e(j)
            before = got_low(y)
            relay_up(y, way_e, before)
            finish(y, before)

        each(first)
        each(second)
        drain((way_b,), (way_c,))
        each(lambda j: finish(row_b(j), got_high(row_b(j))))
        each(lambda j: finish(row_c(j), got_low(row_c(j))))
        drain((way_a, way_e), (way_e,))

    @pl.when(lon == 2)
    def _():
        def first(j):
            y = row_b(j)
            low = got_low(y)
            relay_up(y, way_b, low)
            pass_down(y, way_b)
            finish(y, low + from_high[y, :, :])

        def second(j):
            y = row_a(j)
            before = got_low(y)
            relay_up(y, way_a, before)
            finish(y, before)

        each(first)
        each(second)
        drain((way_c,), (way_e,))
        each(lambda j: finish(row_c(j), got_high(row_c(j))))
        each(lambda j: finish(row_e(j), got_low(row_e(j))))
        drain((way_b, way_a), (way_b,))

    @pl.when(lon == 3)
    def _():
        each(lambda j: pass_down(row_b(j), way_b))
        each(lambda j: pass_down(row_c(j), way_c))

        def both(y):
            finish(y, got_low(y) + from_high[y, :, :])

        each(lambda j: both(row_c(j)))
        each(lambda j: both(row_b(j)))
        each(lambda j: finish(row_e(j), got_high(row_e(j))))
        each(lambda j: finish(row_a(j), got_low(row_a(j))))
        drain((), (way_b, way_c))


def store_kernel(acc, end, acc_out, end_out, sem):
    pairs = ((end, end_out), (acc, acc_out))
    for y in range(acc.shape[0]):
        for i, (src, dst) in enumerate(pairs):
            pltpu.make_async_copy(src.at[y], dst.at[y], sem.at[i]).start()
    for i, (src, dst) in enumerate(pairs):
        pltpu.make_async_copy(src, dst, sem.at[i]).wait()


def per_device(sizes, heat, north, east, up):
    rows, cols, deep, members = heat.shape
    shape = jax.ShapeDtypeStruct(heat.shape, heat.dtype)
    f32 = jnp.float32
    dma = pltpu.SemaphoreType.DMA
    acc, end = pl.pallas_call(
        functools.partial(kernel, sizes),
        out_shape=(shape, shape),
        in_specs=[pl.BlockSpec(memory_space=pl.ANY)] * 4,
        out_specs=(pl.BlockSpec(memory_space=pltpu.VMEM),) * 2,
        scratch_shapes=[
            pltpu.VMEM((2, rows + 2, cols + 2, deep + 2 * PAD, members), f32),
            pltpu.VMEM((3, rows, cols, deep, members), f32),
            pltpu.VMEM((rows, deep, members), f32),
            pltpu.VMEM((rows, deep, members), f32),
            pltpu.VMEM((2, rows, cols, members), f32),
            pltpu.VMEM((2, rows, cols, members), f32),
            dma((2,)),
            dma((3,)),
            dma((2, 2, 4)),
            dma((2, 2, rows)),
            dma((2, 2)),
            dma((2, 2)),
            dma((2, 2)),
            dma((2, 2)),
            dma((2, 4)),
        ],
        compiler_params=pltpu.CompilerParams(
            collective_id=0,
            has_side_effects=True,
            vmem_limit_bytes=40 * 1024 * 1024,
        ),
    )(heat, north, east, up)
    return pl.pallas_call(
        store_kernel,
        out_shape=(shape, shape),
        in_specs=[pl.BlockSpec(memory_space=pltpu.VMEM)] * 2,
        out_specs=(pl.BlockSpec(memory_space=pltpu.HBM),) * 2,
        scratch_shapes=[dma((2,))],
        compiler_params=pltpu.CompilerParams(vmem_limit_bytes=1024 * 1024),
    )(acc, end)


def solution(mesh):
    sizes = tuple(mesh.shape[name] for name in ("lat", "lon", "lev"))
    spec = P("lat", "lon", "lev", None)
    return jax.shard_map(
        functools.partial(per_device, sizes),
        mesh=mesh,
        in_specs=(spec,) * 4,
        out_specs=(spec, spec),
        check_vma=False,
    )
```

time: 127 us -> 124 us (0.976)
  Pallas kernels: 126 us -> 123 us
    pallas_call x1, Pallas kernels: 121 us -> 119 us  [per_device(): pl.pallas_call(functools.partial(kernel, sizes), out_shape=(shape, shape)...]
where the time goes in v4:
time: 124 us
  Pallas kernels  123 us (99%)
    pallas_call x1, Pallas kernels, per_device(): pl.pallas_call(functools.partial(kernel, sizes), out_shape=(shape, shape)...  119 us
    pallas_call x1, Pallas kernels, per_device(): pl.pallas_call(store_kernel, out_shape=(shape, shape), in_specs=[pl.Block...  4.54 us

profile of v4, /device:TPU:120, one launch (start us, length us, event | category | flops | bytes accessed | tf_op | source)
XLA Modules:
  0.0 123.9 jit_solution(14686324285127874164)
XLA Ops:
  0.6 118.7 %shard_map.59 = (f32[16,8,96,128]{3,2,1,0:T(8,128)S(1)}, f32[16,8,96,128]{3,2,1,0:T(8,128)S(1)}) custom-call(f32[16,8,96,128]{3,2,1,0:T(8,128)} %heat.1, f32[16,8,96,128]{3,2,1,0:T(8,128)} %north.1, f32[16,8,96,128]{3,2,1,0:T(8,128)} %east.1, f32[16,8,96,128]{3,2,1,0:T(8,128)} %up.1), custom_call_target="tpu_custom_call" | custom-call | tf_op jit(solution)/shard_map/pallas_call | solution.py:491
  119.3 4.5 %shard_map.60 = (f32[16,8,96,128]{3,2,1,0:T(8,128)}, f32[16,8,96,128]{3,2,1,0:T(8,128)}) custom-call(f32[16,8,96,128]{3,2,1,0:T(8,128)S(1)} %get-tuple-element.4.acc, f32[16,8,96,128]{3,2,1,0:T(8,128)S(1)} %get-tuple-element.5.end), custom_call_target="tpu_custom_call" | custom-call | tf_op jit(solution)/shard_map/pallas_call | solution.py:519

commit v5 on v4

--- a/solution.py
+++ b/solution.py
@@ -40,6 +40,7 @@
     lev_send,
     lev_recv,
     sum_send,
+    sum_recv,
 ):
     lats, lons, levs = sizes
     rows, cols, deep, members = heat.shape
@@ -63,27 +64,38 @@
         return remote(
             field.at[slot, y + 1, (1, cols)[side], body],
             field.at[slot, y + 1, (cols + 1, 0)[side], body],
-            lon_send.at[side, slot, k // quarter],
-            lon_recv.at[side, slot, y],
+            lon_send.at[side, slot, k // half],
+            lon_recv.at[slot, y],
             "lon",
-            lon + (-1, 1)[side],
+            (lon + (lons - 1, 1)[side]) % lons,
         )
 
     def lon_gone(slot, part, side):
-        some = field.at[slot, pl.ds(1, quarter), 1, body]
+        some = field.at[slot, pl.ds(1, half), 1, body]
         remote(
             some,
             some,
             lon_send.at[side, slot, part],
-            lon_recv.at[side, slot, 0],
+            lon_recv.at[slot, 0],
             "lon",
-            lon + (-1, 1)[side],
+            (lon + (lons - 1, 1)[side]) % lons,
         ).wait_send()
+
+    def lon_here(slot, y, count):
+        some = field.at[slot, pl.ds(1, count), 1, body]
+        remote(
+            some,
+            some,
+            lon_send.at[0, slot, 0],
+            lon_recv.at[slot, y],
+            "lon",
+            (lon + 1) % lons,
+        ).wait_recv()
 
     def lat_copy(slot, side):
         src = field.at[slot, (1, rows)[side], pl.ds(1, cols), body]
         dst = field.at[slot, (rows + 1, 0)[side], pl.ds(1, cols), body]
-        to = lat + (-1, 1)[side]
+        to = (lat + (lats - 1, 1)[side]) % lats
         return remote(
             src, dst, lat_send.at[side, slot], lat_recv.at[side, slot], "lat", to
         )
@@ -99,37 +111,33 @@
             1 - lev,
         )
 
+    own_sums, relayed = 0, 1
     spare = STEPS % 2
 
-    def up_copy(y, way, src):
+    def up_copy(y, kind, src):
         return remote(
             src,
             from_low.at[y],
-            sum_send.at[1, way],
-            lon_recv.at[1, spare, y],
+            sum_send.at[kind],
+            lon_recv.at[spare, y],
             "lon",
-            lon + 1,
-        )
-
-    def down_copy(y, way, src):
+            (lon + 1) % lons,
+        )
+
+    def down_copy(y, kind, src):
         return remote(
             src,
             from_high.at[y],
-            sum_send.at[0, way],
-            lon_recv.at[0, spare, y],
+            sum_send.at[kind],
+            sum_recv.at[y],
             "lon",
             (lon + lons - 1) % lons,
         )
 
-    def sums_gone(side, way):
-        some = from_low.at[pl.ds(0, quarter)]
+    def sums_gone(kind, count):
+        some = from_low.at[pl.ds(0, count)]
         remote(
-            some,
-            some,
-            sum_send.at[side, way],
-            lon_recv.at[side, spare, 0],
-            "lon",
-            (lon + (lons - 1, 1)[side]) % lons,
+            some, some, sum_send.at[kind], sum_recv.at[0], "lon", (lon + 1) % lons
         ).wait_send()
 
     lon_has = (lon > 0, lon < lons - 1)
@@ -262,8 +270,10 @@
 
     def arrivals(slot, k):
         y = row_at(k, rows)
+        both = jnp.logical_and(*lon_has)
+        pl.when(both)(lambda: lon_here(slot, y, 2))
+        pl.when(jnp.logical_not(both))(lambda: lon_here(slot, y, 1))
         for side in (0, 1):
-            pl.when(lon_has[side])(lambda: lon_copy(slot, k, 1 - side).wait_recv())
             pl.when(jnp.logical_and(lat_has[side], y == (0, rows - 1)[side]))(
                 lambda: lat_copy(slot, 1 - side).wait_recv()
             )
@@ -272,8 +282,8 @@
     def departures(slot, k):
         y = row_at(k, rows)
         for side in (0, 1):
-            pl.when(jnp.logical_and(lon_has[side], k % quarter == 0))(
-                lambda: lon_gone(slot, k // quarter, side)
+            pl.when(jnp.logical_and(lon_has[side], k % half == 0))(
+                lambda: lon_gone(slot, k // half, side)
             )
             pl.when(jnp.logical_and(lat_has[side], y == (0, rows - 1)[side]))(
                 lambda: lat_copy(slot, side).wait_send()
@@ -314,8 +324,6 @@
     last = (STEPS - 1) % 2
     scale = 1.0 / (cols * lons)
 
-    way_b, way_e, way_a, way_c = range(4)
-
     def row_b(j):
         return row_at(4 * j, rows)
 
@@ -362,8 +370,8 @@
         down_first = jnp.logical_or(
             first(0, 0), jnp.logical_or(first(1, 3), first(2, 1))
         )
-        pl.when(up_first)(lambda: up_copy(y, way, own(y)).start())
-        pl.when(down_first)(lambda: down_copy(y, way, own(y)).start())
+        pl.when(up_first)(lambda: up_copy(y, own_sums, own(y)).start())
+        pl.when(down_first)(lambda: down_copy(y, own_sums, own(y)).start())
         return 0
 
     lax.fori_loop(0, rows, last_row, 0)
@@ -382,17 +390,17 @@
         down_copy(y, 0, own(y)).wait_recv()
         return from_high[y, :, :]
 
-    def relay_up(y, way, value):
+    def relay_up(y, value):
         from_low[y, :, :] = value + acc[y, cols - 1, :, :]
-        up_copy(y, way, from_low.at[y]).start()
-
-    def relay_down(y, way, value):
+        up_copy(y, relayed, from_low.at[y]).start()
+
+    def relay_down(y, value):
         from_high[y, :, :] = value + acc[y, cols - 1, :, :]
-        down_copy(y, way, from_high.at[y]).start()
-
-    def pass_down(y, way):
+        down_copy(y, relayed, from_high.at[y]).start()
+
+    def pass_down(y):
         down_copy(y, 0, own(y)).wait_recv()
-        down_copy(y, way, from_high.at[y]).start()
+        down_copy(y, relayed, from_high.at[y]).start()
 
     def finish(y, before):
         def one(x, _):
@@ -401,68 +409,63 @@
 
         lax.fori_loop(0, cols, one, 0)
 
-    def drain(up, down):
-        for way in up:
-            sums_gone(1, way)
-        for way in down:
-            sums_gone(0, way)
-
     @pl.when(lon == 0)
     def _():
-        each(lambda j: up_copy(row_e(j), way_e, own(row_e(j))).start())
-        each(lambda j: up_copy(row_c(j), way_c, own(row_c(j))).start())
-        each(lambda j: relay_down(row_c(j), way_c, got_high(row_c(j))))
-        each(lambda j: relay_down(row_e(j), way_e, got_high(row_e(j))))
-        drain((way_a, way_e, way_c), (way_b, way_c, way_e))
+        each(lambda j: up_copy(row_e(j), own_sums, own(row_e(j))).start())
+        each(lambda j: up_copy(row_c(j), own_sums, own(row_c(j))).start())
+        each(lambda j: relay_down(row_c(j), got_high(row_c(j))))
+        each(lambda j: relay_down(row_e(j), got_high(row_e(j))))
+        sums_gone(own_sums, 4 * quarter)
+        sums_gone(relayed, 2 * quarter)
 
     @pl.when(lon == 1)
     def _():
         def first(j):
             y = row_a(j)
             before = got_low(y)
-            relay_up(y, way_a, before)
-            relay_down(row_e(j), way_e, got_high(row_e(j)))
+            relay_up(y, before)
+            relay_down(row_e(j), got_high(row_e(j)))
             finish(y, before)
 
         def second(j):
             y = row_e(j)
             before = got_low(y)
-            relay_up(y, way_e, before)
+            relay_up(y, before)
             finish(y, before)
 
         each(first)
         each(second)
-        drain((way_b,), (way_c,))
+        sums_gone(own_sums, 2 * quarter)
         each(lambda j: finish(row_b(j), got_high(row_b(j))))
         each(lambda j: finish(row_c(j), got_low(row_c(j))))
-        drain((way_a, way_e), (way_e,))
+        sums_gone(relayed, 3 * quarter)
 
     @pl.when(lon == 2)
     def _():
         def first(j):
             y = row_b(j)
             low = got_low(y)
-            relay_up(y, way_b, low)
-            pass_down(y, way_b)
+            relay_up(y, low)
+            pass_down(y)
             finish(y, low + from_high[y, :, :])
 
         def second(j):
             y = row_a(j)
             before = got_low(y)
-            relay_up(y, way_a, before)
+            relay_up(y, before)
             finish(y, before)
 
         each(first)
         each(second)
-        drain((way_c,), (way_e,))
+        sums_gone(own_sums, 2 * quarter)
         each(lambda j: finish(row_c(j), got_high(row_c(j))))
         each(lambda j: finish(row_e(j), got_low(row_e(j))))
-        drain((way_b, way_a), (way_b,))
+        sums_gone(relayed, 3 * quarter)
 
     @pl.when(lon == 3)
     def _():
-        each(lambda j: pass_down(row_b(j), way_b))
-        each(lambda j: pass_down(row_c(j), way_c))
+        each(lambda j: pass_down(row_b(j)))
+        each(lambda j: pass_down(row_c(j)))
 
         def both(y):
             finish(y, got_low(y) + from_high[y, :, :])
@@ -471,7 +474,7 @@
         each(lambda j: both(row_b(j)))
         each(lambda j: finish(row_e(j), got_high(row_e(j))))
         each(lambda j: finish(row_a(j), got_low(row_a(j))))
-        drain((), (way_b, way_c))
+        sums_gone(relayed, 2 * quarter)
 
 
 def store_kernel(acc, end, acc_out, end_out, sem):
@@ -502,13 +505,14 @@
             pltpu.VMEM((2, rows, cols, members), f32),
             dma((2,)),
             dma((3,)),
-            dma((2, 2, 4)),
-            dma((2, 2, rows)),
+            dma((2, 2, 2)),
+            dma((2, rows)),
             dma((2, 2)),
             dma((2, 2)),
             dma((2, 2)),
             dma((2, 2)),
-            dma((2, 4)),
+            dma((2,)),
+            dma((rows,)),
         ],
         compiler_params=pltpu.CompilerParams(
             collective_id=0,

time: 124 us -> 124 us (level)
  no operation moved by 1% of the time
where the time goes in v5:
time: 124 us
  Pallas kernels  123 us (99%)
    pallas_call x1, Pallas kernels, per_device(): pl.pallas_call(functools.partial(kernel, sizes), out_shape=(shape, shape)...  119 us
    pallas_call x1, Pallas kernels, per_device(): pl.pallas_call(store_kernel, out_shape=(shape, shape), in_specs=[pl.Block...  4.54 us

profile of v5, /device:TPU:120, one launch (start us, length us, event | category | flops | bytes accessed | tf_op | source)
XLA Modules:
  0.0 123.8 jit_solution(11265593903725399636)
XLA Ops:
  0.6 118.6 %shard_map.59 = (f32[16,8,96,128]{3,2,1,0:T(8,128)S(1)}, f32[16,8,96,128]{3,2,1,0:T(8,128)S(1)}) custom-call(f32[16,8,96,128]{3,2,1,0:T(8,128)} %heat.1, f32[16,8,96,128]{3,2,1,0:T(8,128)} %north.1, f32[16,8,96,128]{3,2,1,0:T(8,128)} %east.1, f32[16,8,96,128]{3,2,1,0:T(8,128)} %up.1), custom_call_target="tpu_custom_call" | custom-call | tf_op jit(solution)/shard_map/pallas_call | solution.py:494
  119.3 4.5 %shard_map.60 = (f32[16,8,96,128]{3,2,1,0:T(8,128)}, f32[16,8,96,128]{3,2,1,0:T(8,128)}) custom-call(f32[16,8,96,128]{3,2,1,0:T(8,128)S(1)} %get-tuple-element.4.acc, f32[16,8,96,128]{3,2,1,0:T(8,128)S(1)} %get-tuple-element.5.end), custom_call_target="tpu_custom_call" | custom-call | tf_op jit(solution)/shard_map/pallas_call | solution.py:523
